TPU v7x, 32 devices: a whole 2x2x4 slice. The times are simulated.
32 devices in a mesh: node: 8 (over z, x), local: 4 (over y, core).
Axes of the slice: x: 2, y: 2, z: 4, core: 2. Of those that a mesh axis runs over, the one named last changes fastest.
Arguments:
- tokens: bfloat16 [2048, 5120], P(('node', 'local')), may hold values from -6 to 6
- node_ids: int32 [2048, 3], P(('node', 'local')), may hold values from 0 to 7, as said below
- expert_ids: int32 [2048, 6], P(('node', 'local')), may hold values from 0 to 23, as said below
- gate_weights: bfloat16 [2048, 6], P(('node', 'local')), may hold values from 0.049804688 to 1
- up_weight: bfloat16 [24, 5120, 1536], P('node', None, 'local'), may hold values from -0.078125 to 0.078125
- down_weight: bfloat16 [24, 1536, 5120], P('node', 'local'), may hold values from -0.15625 to 0.15625
Outputs:
- routed_out: bfloat16 [2048, 5120], P(('node', 'local'))
Inputs may be any that keep to these rules, and one draw needn't show every extreme that they name: `node_ids`: each token names 3 different nodes; the 64 tokens of one device name every node exactly 24 times. Node m holds experts 3 * m to 3 * m + 2. For each j, expert_ids[t, 2 * j] and expert_ids[t, 2 * j + 1] are two different experts of node node_ids[t, j].
All inputs are finite; a program needn't handle non-finite values.
Results may differ from a plain program's by a relative error of at most 0.012.
Values may be sent and summed in bfloat16 or wider, within the bound.
A program may use at most 192 MiB of HBM per device.

v0:
```python
import jax
import jax.numpy as jnp
from jax import lax
from jax.sharding import PartitionSpec as P


def body(tokens, node_ids, expert_ids, gate_weights, up_weight, down_weight):
    tok_rows, model_width = tokens.shape
    node_count = lax.axis_size("node")
    per_node = up_weight.shape[0]
    capacity = node_ids.shape[1] * tok_rows // node_count
    slot_count = node_count * capacity
    node_grid = jnp.arange(node_count, dtype=jnp.int32)
    picked = jnp.any(node_ids[:, :, None] == node_grid[None, None, :], axis=1).astype(jnp.int32)
    rank_rows = jnp.cumsum(picked, axis=0) - picked
    target = jnp.where(picked > 0, node_grid[None, :] * capacity + rank_rows, -1)
    slot_grid = jnp.arange(slot_count, dtype=jnp.int32)
    placing = (jnp.repeat(target, capacity, axis=1) == slot_grid[None, :]).astype(jnp.bfloat16)
    expert_grid = jnp.arange(node_count * per_node, dtype=jnp.int32)
    flat_gates = jnp.sum(
        jnp.where(
            expert_ids[:, :, None] == expert_grid[None, None, :],
            gate_weights.astype(jnp.float32)[:, :, None],
            0.0,
        ),
        axis=1,
    )
    by_node = jnp.repeat(flat_gates.reshape(tok_rows, node_count, per_node), capacity, axis=1)
    slot_gates = jnp.einsum(
        "ts,tse->se", placing.astype(jnp.float32), by_node, precision=lax.Precision.HIGHEST
    )
    outgoing = lax.dot_general(
        placing, tokens, (((0,), (0,)), ((), ())), preferred_element_type=jnp.float32
    ).astype(jnp.bfloat16)
    arrived, arrived_gates = (
        lax.all_to_all(
            outgoing.reshape(node_count, capacity, model_width),
            "node",
            split_axis=0,
            concat_axis=0,
            tiled=True,
        ),
        lax.all_to_all(
            slot_gates.astype(jnp.bfloat16).reshape(node_count, capacity, per_node),
            "node",
            split_axis=0,
            concat_axis=0,
            tiled=True,
        ),
    )
    arrived = arrived.reshape(slot_count, model_width)
    arrived_gates = arrived_gates.reshape(slot_count, per_node)
    pooled, pooled_gates = (
        lax.all_gather(arrived, "local", axis=0, tiled=True),
        lax.all_gather(arrived_gates, "local", axis=0, tiled=True),
    )
    rows_gate = pooled_gates.astype(jnp.float32)
    running = jnp.zeros((slot_count * lax.axis_size("local"), model_width), jnp.float32)
    for expert in range(per_node):
        lifted = jnp.dot(pooled, up_weight[expert], preferred_element_type=jnp.float32)
        scaled = (jax.nn.silu(lifted) * rows_gate[:, expert : expert + 1]).astype(jnp.bfloat16)
        running = running + jnp.dot(scaled, down_weight[expert], preferred_element_type=jnp.float32)
    summed = lax.psum_scatter(
        running.astype(jnp.bfloat16).astype(jnp.float32).astype(jnp.bfloat16),
        "local",
        scatter_dimension=0,
        tiled=True,
    )
    returned = lax.all_to_all(
        summed.reshape(node_count, capacity, model_width),
        "node",
        split_axis=0,
        concat_axis=0,
        tiled=True,
    )
    combined = jnp.dot(
        placing, returned.reshape(slot_count, model_width), preferred_element_type=jnp.float32
    )
    return combined.astype(jnp.bfloat16)


def solution(mesh):
    in_specs = (
        P(("node", "local"), None),
        P(("node", "local"), None),
        P(("node", "local"), None),
        P(("node", "local"), None),
        P("node", None, "local"),
        P("node", "local", None),
    )
    out_specs = P(("node", "local"), None)
    return jax.shard_map(body, mesh=mesh, in_specs=in_specs, out_specs=out_specs, check_vma=False)
```

profile of v0, /device:TPU:9, one launch (start us, length us, event | category | flops | bytes accessed | tf_op | source)
XLA Modules:
  0.0 296.3 jit_solution(15938106576258352738)
XLA Ops:
  6.5 0.0 copy-start
  6.5 0.0 all-gather.3.cloned.1.call-start
  6.5 0.8 fusion.42
  7.3 0.1 copy.54
  7.4 0.1 reduce_window_sum.11
  7.5 0.1 copy.55
  7.6 0.0 copy-done
  7.6 0.0 copy-start.2
  7.7 0.7 convolution_convert_fusion
  8.3 49.8 %all_to_all.15 = bf16[8,24,5120]{2,1,0:T(8,128)(2,1)} all-to-all(bf16[8,24,5120]{2,1,0:T(8,128)(2,1)S(1)} %bitcast.58), channel_id=1, replica_groups=mesh['node'=8,'local'=4] {'node'}, dimensions={0} | all-to-all | bytes 3932160 | tf_op jit(solution)/shard_map/all_to_all | solution.py:36
  58.2 0.0 all-gather.3.cloned.1.call-update
  58.2 0.0 reduce-scatter.2.cloned.1.call-start
  58.2 0.0 copy-done.3
  58.2 0.0 copy-done.2
  58.3 0.9 fusion.36
  59.2 0.1 copy.62
  59.3 0.1 reshape.48
  59.5 8.5 %all_to_all.16 = bf16[8,24,3]{1,2,0:T(4,128)(2,1)S(1)} all-to-all(bf16[8,24,3]{1,2,0:T(4,128)(2,1)S(1)} %copy.57), channel_id=1, replica_groups=mesh['node'=8,'local'=4] {'node'}, dimensions={0} | all-to-all | bytes 2304 | tf_op jit(solution)/shard_map/all_to_all | solution.py:43
  68.0 0.1 reshape.51
  68.1 7.5 %all-gather = bf16[4,192,3]{1,2,0:T(4,128)(2,1)S(1)} all-gather(bf16[1,192,3]{1,2,0:T(4,128)(2,1)S(1)} %reshape.51), channel_id=1, replica_groups=mesh['node'=8,'local'=4] {'local'}, dimensions={0}, use_global_device_ids=true | all-gather | bytes 5760 | tf_op jit(solution)/shard_map/all_gather | solution.py:55
  75.6 0.1 reshape.53
  75.7 38.6 %all-gather.3.cloned.1.call-done = bf16[768,5120]{1,0:T(8,128)(2,1)} async-done(((bf16[192,5120]{1,0:T(8,128)(2,1)}), bf16[768,5120]{1,0:T(8,128)(2,1)}) %all-gather.3.cloned.1.call-update) | async-done | bytes 7864336 | tf_op jit(solution)/shard_map/all_gather | solution.py:54
  114.3 16.3 %fusion.4 = f32[768,5120]{1,0:T(8,128)} fusion(bf16[3,384,5120]{2,1,0:T(8,128)(2,1)} %param.11, bf16[768,5120]{1,0:T(8,128)(2,1)} %all-gather.3.cloned.1.call-done, bf16[3,5120,384]{2,1,0:T(8,128)(2,1)} %param.10, f32[768]{0:T(1024)S(1)} %get-tuple-element.6), kind=kOutput, calls=%fused_computation.7 | convolution fusion | flops 6041567232 | bytes 31460352 | tf_op jit(solution)/shard_map/dot_general | solution.py:62
  130.6 16.3 %fusion.8 = f32[768,5120]{1,0:T(8,128)} fusion(bf16[3,384,5120]{2,1,0:T(8,128)(2,1)} %param.11, bf16[768,5120]{1,0:T(8,128)(2,1)} %all-gather.3.cloned.1.call-done, bf16[3,5120,384]{2,1,0:T(8,128)(2,1)} %param.10, f32[768]{0:T(1024)S(1)} %get-tuple-element.7), kind=kOutput, calls=%fused_computation.11 | convolution fusion | flops 6041567232 | bytes 31460352 | tf_op jit(solution)/shard_map/dot_general | solution.py:62
  146.9 22.9 %add_convert_fusion = bf16[768,5120]{1,0:T(8,128)(2,1)} fusion(f32[768,5120]{1,0:T(8,128)} %fusion.8, f32[768,5120]{1,0:T(8,128)} %fusion.4, bf16[3,384,5120]{2,1,0:T(8,128)(2,1)} %param.11, bf16[768,5120]{1,0:T(8,128)(2,1)} %all-gather.3.cloned.1.call-done, bf16[3,5120,384]{2,1,0:T(8,128)(2,1)} %param.10, f32[768]{0:T(1024)S(1)} %get-tuple-element.5), kind=kOutput, calls=%fused_computation | convolution fusion | flops 6053363712 | bytes 55053312 | tf_op jit(solution)/shard_map/dot_general | solution.py:62
  169.8 0.0 reduce-scatter.2.cloned.1.call-update
  169.8 0.0 copy-start.1
  169.8 69.0 %reduce-scatter.2.cloned.1.call-done = bf16[192,5120]{1,0:T(8,128)(2,1)} async-done(((bf16[768,5120]{1,0:T(8,128)(2,1)}), bf16[192,5120]{1,0:T(8,128)(2,1)}) %reduce-scatter.2.cloned.1.call-update) | async-done | bytes 1966096 | tf_op jit(solution)/shard_map/reduce_scatter | solution.py:63
  238.8 5.5 %all-to-all-start.2 = ((bf16[8,24,5120]{2,1,0:T(8,128)(2,1)}), bf16[8,24,5120]{2,1,0:T(8,128)(2,1)S(1)}, u32[]{:S(2)}, u32[]{:S(2)}) async-start(bf16[8,24,5120]{2,1,0:T(8,128)(2,1)} %bitcast.60), calls=%async_computation.3 | async-start | bytes 3932160 | tf_op jit(solution)/shard_map/all_to_all | solution.py:69
  244.4 43.7 %all-to-all-done.2 = bf16[8,24,5120]{2,1,0:T(8,128)(2,1)S(1)} async-done(((bf16[8,24,5120]{2,1,0:T(8,128)(2,1)}), bf16[8,24,5120]{2,1,0:T(8,128)(2,1)S(1)}, u32[]{:S(2)}, u32[]{:S(2)}) %all-to-all-start.2) | async-done | bytes 1966112 | tf_op jit(solution)/shard_map/all_to_all | solution.py:69
  288.1 1.4 fusion
  289.5 0.0 copy-done.1
  (15 shorter events, 0.2 us)
Async XLA Ops:
  6.5 1.1 copy-start
  6.5 107.8 %all-gather.3.cloned.1.call-start = ((), (), s32[]{:S(2)}) async-start(), calls=%async_computation.4 | async-start | bytes 9830400 | tf_op jit(solution)/shard_map/all_gather | solution.py:54
  7.6 50.6 %copy-start.3 = (bf16[64,6]{0,1:T(8,128)(2,1)S(1)}, bf16[64,6]{0,1:T(8,128)(2,1)}, u32[]{:S(2)}) copy-start(bf16[64,6]{0,1:T(8,128)(2,1)} %param.9) | copy-start | bytes 2308
  7.6 50.6 %copy-start.2 = (s32[64,6]{0,1:T(8,128)S(1)}, s32[64,6]{0,1:T(8,128)}, u32[]{:S(2)}) copy-start(s32[64,6]{0,1:T(8,128)} %param.8) | copy-start | bytes 4612
  58.2 180.7 %reduce-scatter.2.cloned.1.call-start = ((), (), s32[]{:S(2)}) async-start(), calls=%async_computation.5 | async-start | bytes 9830400 | tf_op jit(solution)/shard_map/reduce_scatter | solution.py:63
  169.8 119.7 %copy-start.1 = (bf16[64,5120]{1,0:T(8,128)(2,1)S(1)}, bf16[64,5120]{1,0:T(8,128)(2,1)}, u32[]{:S(2)}) copy-start(bf16[64,5120]{1,0:T(8,128)(2,1)} %param.6) | copy-start | bytes 1966084
  238.8 49.2 %all-to-all-start.2 = ((bf16[8,24,5120]{2,1,0:T(8,128)(2,1)}), bf16[8,24,5120]{2,1,0:T(8,128)(2,1)S(1)}, u32[]{:S(2)}, u32[]{:S(2)}) async-start(bf16[8,24,5120]{2,1,0:T(8,128)(2,1)} %bitcast.60), calls=%async_computation.3 | async-start | bytes 3932160 | tf_op jit(solution)/shard_map/all_to_all | solution.py:69
Sparse Core Ops, SparseCore 0:
  58.3 55.9 all-gather.2
  169.9 68.8 reduce-scatter.1
where the time goes:
time: 300 us; the launch traced here: 296 us
  waiting for transfers between devices  151 us (50%)
  blocking collectives  65.9 us (22%)
  matrix products  58.4 us (19%)
  between operations  13.5 us (4%)
  starting transfers between devices  5.55 us (2%)
    reduce_scatter x1, waiting for transfers between devices, body(): lax.psum_scatter(running.astype(jnp.bfloat16).astype(jnp.float32).astype(...  69 us
    dot_general x3, matrix products, body(): jnp.dot(scaled, down_weight[expert], preferred_element_type=jnp.float32)  55.4 us
    all_to_all x1, blocking collectives, body(): lax.all_to_all(outgoing.reshape(node_count, capacity, model_width), 'node...  49.8 us
    all_to_all x1, waiting for transfers between devices, body(): lax.all_to_all(summed.reshape(node_count, capacity, model_width), 'node',...  43.7 us
    all_gather x1, waiting for transfers between devices, body(): lax.all_gather(arrived, 'local', axis=0, tiled=True)  38.6 us
    all_to_all x1, blocking collectives, body(): lax.all_to_all(slot_gates.astype(jnp.bfloat16).reshape(node_count, capaci...  8.55 us
    all_gather x1, blocking collectives, body(): lax.all_gather(arrived_gates, 'local', axis=0, tiled=True)  7.47 us
  transfers between devices with their start and end apart: 3, of which 3 were waited for; matrix products, arithmetic and copies ran while one was open for 0% of the time, Pallas kernels for 0%

commit v1 on v0

v1 whole, which is shorter than its diff:
```python
import functools

import jax
import jax.numpy as jnp
from jax import lax
from jax.experimental import pallas as pl
from jax.experimental.pallas import tpu as pltpu
from jax.sharding import PartitionSpec as P

GROUPS = 4
LANES = 128
MESH = pl.DeviceIdType.MESH


def partner(index, step, bits):
    total = 0
    for b in range(bits):
        w = 1 << b
        total = total + ((index // w + step // w) % 2) * w
    return total


def dot(a, b):
    return jnp.dot(a, b, preferred_element_type=jnp.float32)


def kernel(
    cfg,
    tok_ref, nid_ref, eid_ref, gate_ref, up_hbm, down_hbm,
    out_ref,
    up, down, toks, ext, ext_own, packed, rx, px, hid, p_own, p_oth, pr, yr, back, place, final,
    w_sem, x_send, x_recv, a_send, a_recv, y_send, y_recv, d_send, d_recv,
    e_send, e_recv, c_send, c_recv, b_send, b_recv, f_send, f_recv,
):
    n, bits, cap, blk, rows, half, width, per_node, unit, chunk = cfg
    gs = n // GROUPS
    gh = gs * blk
    quota = n * blk
    node = lax.axis_index("node")
    loc = lax.axis_index("local")
    hi, lo = loc // 2, loc % 2
    lo_peer = (node, hi * 2 + (1 - lo))
    hi_peer = (node, (1 - hi) * 2 + lo)

    def remote(src, dst, ssem, rsem, dev):
        return pltpu.make_async_remote_copy(
            src_ref=src, dst_ref=dst, send_sem=ssem, recv_sem=rsem,
            device_id=dev, device_id_type=MESH,
        )

    up_copy = pltpu.make_async_copy(up_hbm, up, w_sem.at[0])
    down_copy = pltpu.make_async_copy(down_hbm, down, w_sem.at[1])
    up_copy.start()
    down_copy.start()

    barrier = pltpu.get_barrier_semaphore()
    for s in range(1, n):
        pl.semaphore_signal(barrier, inc=1, device_id=(partner(node, s, bits), loc), device_id_type=MESH)
    pl.semaphore_signal(barrier, inc=1, device_id=lo_peer, device_id_type=MESH)
    pl.semaphore_signal(barrier, inc=1, device_id=hi_peer, device_id_type=MESH)

    k_sel = nid_ref.shape[1]
    k_top = eid_ref.shape[1]
    lane_r = lax.broadcasted_iota(jnp.int32, (rows, LANES), 1)
    facts = jnp.zeros((rows, LANES), jnp.float32)
    nid = nid_ref[...].astype(jnp.float32)
    eid = eid_ref[...].astype(jnp.float32)
    gat = gate_ref[...].astype(jnp.float32)
    for j in range(k_sel):
        facts = jnp.where(lane_r == j, nid[:, j : j + 1], facts)
    for j in range(k_top):
        facts = jnp.where(lane_r == k_sel + j, eid[:, j : j + 1], facts)
        facts = jnp.where(lane_r == k_sel + k_top + j, gat[:, j : j + 1], facts)
    mine = pl.ds(pl.multiple_of(lo * rows, rows), rows)
    ext_own[...] = facts.astype(jnp.bfloat16)
    my_cols = pl.ds(pl.multiple_of(lo * half, LANES), half)
    peer_cols = pl.ds(pl.multiple_of((1 - lo) * half, LANES), half)

    pl.semaphore_wait(barrier, n + 1)
    ext_copy = remote(ext_own, ext.at[mine], x_send.at[0], x_recv.at[0], lo_peer)
    ext_copy.start()
    tok_copy = remote(tok_ref.at[:, peer_cols], toks.at[mine], x_send.at[1], x_recv.at[1], lo_peer)
    tok_copy.start()
    ext[mine, :] = facts.astype(jnp.bfloat16)
    toks[mine, :] = tok_ref[:, my_cols]
    ext_copy.wait()

    both = 2 * rows
    f = ext[...].astype(jnp.float32)
    lane = lax.broadcasted_iota(jnp.int32, (both, LANES), 1)
    row = lax.broadcasted_iota(jnp.int32, (both, LANES), 0)
    nlane = jnp.where(lane < n, jnp.bitwise_xor(lane, node), -1).astype(jnp.float32)
    picked = jnp.zeros((both, LANES), jnp.float32)
    for j in range(k_sel):
        picked = picked + jnp.where(f[:, j : j + 1] == nlane, 1.0, 0.0)
    tr = lax.broadcasted_iota(jnp.int32, (both, both), 0)
    tc = lax.broadcasted_iota(jnp.int32, (both, both), 1)
    earlier = jnp.where((tc < tr) & ((tc >= rows) == (tr >= rows)), 1.0, 0.0).astype(jnp.bfloat16)
    rank = dot(earlier, picked.astype(jnp.bfloat16))
    slot = rank + jnp.where(row >= rows, float(cap), 0.0)
    slot1 = jnp.where(picked > 0.0, slot + 1.0, 0.0).astype(jnp.bfloat16)
    rq = lax.broadcasted_iota(jnp.int32, (LANES, quota), 1)
    rn = lax.broadcasted_iota(jnp.int32, (LANES, quota), 0) * blk
    spread = jnp.where((rq >= rn) & (rq < rn + blk), 1.0, 0.0).astype(jnp.bfloat16)
    rep = dot(slot1, spread)
    qf = lax.broadcasted_iota(jnp.int32, (both, quota), 1).astype(jnp.float32)
    qslot = qf - jnp.floor((qf + 0.5) * (1.0 / blk)) * blk
    placing = jnp.where(rep == qslot + 1.0, 1.0, 0.0)
    place[...] = placing.astype(jnp.bfloat16)
    placing_t = jnp.transpose(placing).astype(jnp.bfloat16)

    qrow = lax.broadcasted_iota(jnp.int32, (quota, LANES), 0)
    qlane = lax.broadcasted_iota(jnp.int32, (quota, LANES), 1)
    ql = qlane * blk
    own_lane = (qrow >= ql) & (qrow < ql + blk)
    slot_gates = jnp.zeros((quota, LANES), jnp.float32)
    for e in range(per_node):
        g = jnp.zeros((both, LANES), jnp.float32)
        for k in range(k_top):
            hit = (f[:, k_sel + k : k_sel + k + 1] == nlane * per_node + e) & (lane < n)
            g = g + jnp.where(hit, f[:, k_sel + k_top + k : k_sel + k_top + k + 1], 0.0)
        picked_gate = dot(placing_t, g.astype(jnp.bfloat16))
        col = jnp.sum(jnp.where(own_lane, picked_gate, 0.0), axis=1, keepdims=True)
        slot_gates = jnp.where(qlane == e, col, slot_gates)
    packed[:, half:] = slot_gates.astype(jnp.bfloat16)

    tok_copy.wait()

    def pack(j, carry):
        cols = pl.ds(pl.multiple_of(j * chunk, LANES), chunk)
        packed[:, cols] = dot(placing_t, toks[:, cols]).astype(jnp.bfloat16)
        return carry

    lax.fori_loop(0, half // chunk, pack, 0)

    def a_copy(s):
        g, j = s // gs, s % gs
        return remote(
            packed.at[pl.ds(s * blk, blk)], rx.at[g, pl.ds(j * blk, blk)],
            a_send.at[s], a_recv.at[s], (partner(node, s, bits), loc),
        )

    for s in range(1, n):
        a_copy(s).start()
    rx[0, :blk, :] = packed[:blk, :]

    def y_copy(g):
        return remote(rx.at[g, pl.ds(0, gh)], rx.at[g, pl.ds(gh, gh)], y_send.at[g], y_recv.at[g], hi_peer)

    def d_copy(g, k):
        part = pl.ds(k * gh, gh)
        return remote(
            rx.at[g, part, pl.ds(0, half)], px.at[g, part],
            d_send.at[2 * g + k], d_recv.at[2 * g + k], lo_peer,
        )

    def fwd(g):
        for s in range(max(1, g * gs), (g + 1) * gs):
            a_copy(s).wait_recv()
        y_copy(g).start()
        d_copy(g, 0).start()

    def rel(g):
        y_copy(g).wait_recv()
        d_copy(g, 1).start()

    def e_copy(g):
        return remote(p_oth.at[g], pr.at[g], e_send.at[g], e_recv.at[g], lo_peer)

    def c_copy(g):
        return remote(p_own.at[g, pl.ds(gh, gh)], yr.at[g], c_send.at[g], c_recv.at[g], hi_peer)

    def b_copy(s):
        g, j = s // gs, s % gs
        return remote(
            p_own.at[g, pl.ds(j * blk, blk)], back.at[pl.ds(s * blk, blk)],
            b_send.at[s], b_recv.at[s], (partner(node, s, bits), loc),
        )

    glane = lax.broadcasted_iota(jnp.int32, (2 * gh, LANES), 1)

    def compute(g):
        d_copy(g, 0).wait_recv()
        d_copy(g, 1).wait_recv()
        gates = rx[g, :, half:].astype(jnp.float32)
        my_k = pl.ds(pl.multiple_of(lo * half, LANES), half)
        peer_k = pl.ds(pl.multiple_of((1 - lo) * half, LANES), half)

        def one(e, carry):
            lifted = dot(rx[g, :, :half], up[e, my_k, :]) + dot(px[g], up[e, peer_k, :])
            gate = jnp.sum(jnp.where(glane == e, gates, 0.0), axis=1, keepdims=True)
            scaled = lifted / (1.0 + jnp.exp(-lifted)) * gate
            hid[:, pl.ds(pl.multiple_of(e * unit, LANES), unit)] = scaled.astype(jnp.bfloat16)
            return carry

        lax.fori_loop(0, per_node, one, 0)

    def lower(g, dst, base):
        def one(j, carry):
            src = pl.ds(pl.multiple_of(base + j * chunk, LANES), chunk)
            cols = pl.ds(pl.multiple_of(j * chunk, LANES), chunk)
            dst[g, :, cols] = dot(hid[...], down[:, src]).astype(jnp.bfloat16)
            return carry

        lax.fori_loop(0, half // chunk, one, 0)

    def project(g):
        lower(g, p_oth, (1 - lo) * half)
        e_copy(g).start()
        lower(g, p_own, lo * half)

    def add_into(dst, g, part, src):
        def one(j, carry):
            cols = pl.ds(pl.multiple_of(j * chunk, LANES), chunk)
            total = dst[g, part, cols].astype(jnp.float32) + src[g, part, cols].astype(jnp.float32)
            dst[g, part, cols] = total.astype(jnp.bfloat16)
            return carry

        lax.fori_loop(0, half // chunk, one, 0)

    def comb1(g):
        e_copy(g).wait_recv()
        add_into(p_own, g, slice(gh, 2 * gh), pr)
        c_copy(g).start()
        add_into(p_own, g, slice(0, gh), pr)

    def comb2(g):
        c_copy(g).wait_recv()
        add_into(p_own, g, slice(0, gh), yr)
        for s in range(max(1, g * gs), (g + 1) * gs):
            b_copy(s).start()
        if g == 0:
            back[:blk, :] = p_own[0, :blk, :]

    fwd(0)
    fwd(1)
    rel(0)
    rel(1)
    up_copy.wait()
    down_copy.wait()
    fwd(2)
    compute(1)
    project(1)
    comb1(1)
    fwd(3)
    rel(2)
    compute(2)
    project(2)
    comb2(1)
    comb1(2)
    rel(3)
    compute(3)
    project(3)
    comb2(2)
    comb1(3)
    compute(0)
    project(0)
    comb1(0)
    comb2(3)
    comb2(0)

    for s in range(1, n):
        b_copy(s).wait_recv()

    def merge(j, carry):
        cols = pl.ds(pl.multiple_of(j * chunk, LANES), chunk)
        final[:, cols] = dot(place[...], back[:, cols]).astype(jnp.bfloat16)
        return carry

    lax.fori_loop(0, half // chunk, merge, 0)
    theirs = pl.ds(pl.multiple_of((1 - lo) * rows, rows), rows)
    f_copy = remote(final.at[theirs], out_ref.at[:, my_cols], f_send.at[0], f_recv.at[0], lo_peer)
    f_copy.start()
    out_ref[:, my_cols] = final[mine, :]

    for s in range(1, n):
        a_copy(s).wait_send()
        b_copy(s).wait_send()
    for g in range(GROUPS):
        y_copy(g).wait_send()
        d_copy(g, 0).wait_send()
        d_copy(g, 1).wait_send()
        e_copy(g).wait_send()
        c_copy(g).wait_send()
    f_copy.wait()


def body(tokens, node_ids, expert_ids, gate_weights, up_weight, down_weight):
    rows, model_width = tokens.shape
    n = lax.axis_size("node")
    per_node, _, unit = up_weight.shape
    cap = node_ids.shape[1] * rows // n
    blk = -(-2 * cap // 16) * 16
    half = model_width // 2
    width = half + LANES
    bits = n.bit_length() - 1
    chunk = next(c for c in (512, 256, 128) if half % c == 0)
    gs = n // GROUPS
    gr = 2 * gs * blk
    cfg = (n, bits, cap, blk, rows, half, width, per_node, unit, chunk)
    bf = jnp.bfloat16
    dma = pltpu.SemaphoreType.DMA
    vmem = pl.BlockSpec(memory_space=pltpu.VMEM)
    hbm = pl.BlockSpec(memory_space=pl.ANY)
    return pl.pallas_call(
        functools.partial(kernel, cfg),
        out_shape=jax.ShapeDtypeStruct((rows, model_width), bf),
        in_specs=[vmem, vmem, vmem, vmem, hbm, hbm],
        out_specs=vmem,
        scratch_shapes=[
            pltpu.VMEM(up_weight.shape, bf),
            pltpu.VMEM((per_node * unit, model_width), bf),
            pltpu.VMEM((2 * rows, half), bf),
            pltpu.VMEM((2 * rows, LANES), bf),
            pltpu.VMEM((rows, LANES), bf),
            pltpu.VMEM((n * blk, width), bf),
            pltpu.VMEM((GROUPS, gr, width), bf),
            pltpu.VMEM((GROUPS, gr, half), bf),
            pltpu.VMEM((gr, per_node * unit), bf),
            pltpu.VMEM((GROUPS, gr, half), bf),
            pltpu.VMEM((GROUPS, gr, half), bf),
            pltpu.VMEM((GROUPS, gr, half), bf),
            pltpu.VMEM((GROUPS, gr // 2, half), bf),
            pltpu.VMEM((n * blk, half), bf),
            pltpu.VMEM((2 * rows, n * blk), bf),
            pltpu.VMEM((2 * rows, half), bf),
            dma((2,)),
            dma((2,)), dma((2,)),
            dma((n,)), dma((n,)),
            dma((GROUPS,)), dma((GROUPS,)),
            dma((2 * GROUPS,)), dma((2 * GROUPS,)),
            dma((GROUPS,)), dma((GROUPS,)),
            dma((GROUPS,)), dma((GROUPS,)),
            dma((n,)), dma((n,)),
            dma((1,)), dma((1,)),
        ],
        compiler_params=pltpu.CompilerParams(
            collective_id=0, has_side_effects=True, vmem_limit_bytes=67043328
        ),
    )(
        tokens, node_ids, expert_ids, gate_weights, up_weight,
        down_weight.reshape(per_node * unit, model_width),
    )


def solution(mesh):
    in_specs = (
        P(("node", "local"), None),
        P(("node", "local"), None),
        P(("node", "local"), None),
        P(("node", "local"), None),
        P("node", None, "local"),
        P("node", "local", None),
    )
    out_specs = P(("node", "local"), None)
    return jax.shard_map(body, mesh=mesh, in_specs=in_specs, out_specs=out_specs, check_vma=False)
```

time: 300 us -> 138 us (0.46); the launches traced: 296 us -> 138 us
  waiting for transfers between devices: 151 us -> 0 us
  Pallas kernels: 0 us -> 132 us
  blocking collectives: 65.9 us -> 0 us
  matrix products: 58.4 us -> 0 us
  between operations: 13.5 us -> 0.01 us
  starting transfers between devices: 5.55 us -> 0 us
  local copies, waits for them, and re-layouts: 0.65 us -> 6.1 us
    pallas_call x0 -> x1, Pallas kernels: none -> 132 us  [body(): pl.pallas_call(functools.partial(kernel, cfg), out_shape=jax.ShapeDtypeSt...]
    reduce_scatter x1 -> x0, waiting for transfers between devices: 69 us -> none  [body(): lax.psum_scatter(running.astype(jnp.bfloat16).astype(jnp.float32).astype(...]
    dot_general x6 -> x0, matrix products: 58.4 us -> none  [the longest x3 55.4 us: body(): jnp.dot(scaled, down_weight[expert], preferred_element_type=jnp.float32)]
    all_to_all x2 -> x0, blocking collectives: 58.4 us -> none  [the longest x1 49.8 us: body(): lax.all_to_all(outgoing.reshape(node_count, capacity, model_width), 'node...]
    all_to_all x1 -> x0, waiting for transfers between devices: 43.7 us -> none  [body(): lax.all_to_all(summed.reshape(node_count, capacity, model_width), 'node',...]
    all_gather x1 -> x0, waiting for transfers between devices: 38.6 us -> none  [body(): lax.all_gather(arrived, 'local', axis=0, tiled=True)]
    all_gather x1 -> x0, blocking collectives: 7.47 us -> none  [body(): lax.all_gather(arrived_gates, 'local', axis=0, tiled=True)]
    unnamed x9 -> x4, local copies, waits for them, and re-layouts: 0.12 us -> 6.1 us
  transfers between devices with their start and end apart: 3 -> 0, of which waited for: 3 -> 0; matrix products, arithmetic and copies ran while one was open for 0% -> 0% of each run, Pallas kernels for 0% -> 0%
where the time goes in v1:
time: 138 us
  Pallas kernels  132 us (96%)
  local copies, waits for them, and re-layouts  6.1 us (4%)
    pallas_call x1, Pallas kernels, body(): pl.pallas_call(functools.partial(kernel, cfg), out_shape=jax.ShapeDtypeSt...  132 us
    unnamed x4, local copies, waits for them, and re-layouts  6.1 us

profile of v1, /device:TPU:9, one launch (start us, length us, event | category | flops | bytes accessed | tf_op | source)
XLA Modules:
  0.0 137.9 jit_solution(275750692152313820)
XLA Ops:
  0.0 1.4 copy.9.gate_ref
  1.4 1.4 %copy.7.nid_ref = s32[64,3]{1,0:T(8,128)} copy(s32[64,3]{0,1:T(4,128)} %param.7) | data formatting | bytes 1536 | tf_op args[1]
  2.8 1.4 copy.8.eid_ref
  4.1 131.8 %shard_map.64 = bf16[64,5120]{1,0:T(8,128)(2,1)} custom-call(bf16[64,5120]{1,0:T(8,128)(2,1)} %tok_ref.1, s32[64,3]{1,0:T(8,128)} %copy.7.nid_ref, s32[64,6]{1,0:T(8,128)} %copy.8.eid_ref, bf16[64,6]{1,0:T(8,128)(2,1)} %copy.9.gate_ref, bf16[3,5120,384]{2,1,0:T(8,128)(2,1)} %up_hbm.1, bf16[1152,5120]{1,0:T(8,128)(2,1)} %bitcast.1), custom_call_target="tpu_custom_call" | custom-call | tf_op jit(solution)/shard_map/pallas_call | solution.py:305
  135.9 2.0 %copy.11 = bf16[64,5120]{1,0:T(8,128)(2,1)} copy(bf16[64,5120]{1,0:T(8,128)(2,1)} %shard_map.64) | data formatting | bytes 1310720

commit v2 on v1

--- a/solution.py
+++ b/solution.py
@@ -35,6 +35,8 @@
     n, bits, cap, blk, rows, half, width, per_node, unit, chunk = cfg
     gs = n // GROUPS
     gh = gs * blk
+    hb = gs // 2
+    uh = hb * blk
     quota = n * blk
     node = lax.axis_index("node")
     loc = lax.axis_index("local")
@@ -59,18 +61,19 @@
     pl.semaphore_signal(barrier, inc=1, device_id=lo_peer, device_id_type=MESH)
     pl.semaphore_signal(barrier, inc=1, device_id=hi_peer, device_id_type=MESH)
 
-    k_sel = nid_ref.shape[1]
-    k_top = eid_ref.shape[1]
-    lane_r = lax.broadcasted_iota(jnp.int32, (rows, LANES), 1)
-    facts = jnp.zeros((rows, LANES), jnp.float32)
+    k_sel = nid_ref.shape[0]
+    k_top = eid_ref.shape[0]
+    line = lax.broadcasted_iota(jnp.int32, (LANES, rows), 0)
+    facts = jnp.zeros((LANES, rows), jnp.float32)
     nid = nid_ref[...].astype(jnp.float32)
     eid = eid_ref[...].astype(jnp.float32)
     gat = gate_ref[...].astype(jnp.float32)
     for j in range(k_sel):
-        facts = jnp.where(lane_r == j, nid[:, j : j + 1], facts)
+        facts = jnp.where(line == j, nid[j : j + 1, :], facts)
     for j in range(k_top):
-        facts = jnp.where(lane_r == k_sel + j, eid[:, j : j + 1], facts)
-        facts = jnp.where(lane_r == k_sel + k_top + j, gat[:, j : j + 1], facts)
+        facts = jnp.where(line == k_sel + j, eid[j : j + 1, :], facts)
+        facts = jnp.where(line == k_sel + k_top + j, gat[j : j + 1, :], facts)
+    facts = jnp.transpose(facts)
     mine = pl.ds(pl.multiple_of(lo * rows, rows), rows)
     ext_own[...] = facts.astype(jnp.bfloat16)
     my_cols = pl.ds(pl.multiple_of(lo * half, LANES), half)
@@ -140,12 +143,18 @@
             a_send.at[s], a_recv.at[s], (partner(node, s, bits), loc),
         )
 
-    for s in range(1, n):
+    for s in range(1, n // 2):
         a_copy(s).start()
+        a_copy(s + n // 2 - 1).start()
+    a_copy(n - 1).start()
     rx[0, :blk, :] = packed[:blk, :]
 
-    def y_copy(g):
-        return remote(rx.at[g, pl.ds(0, gh)], rx.at[g, pl.ds(gh, gh)], y_send.at[g], y_recv.at[g], hi_peer)
+    def y_copy(u):
+        g, base = u // 2, (u % 2) * uh
+        return remote(
+            rx.at[g, pl.ds(base, uh)], rx.at[g, pl.ds(gh + base, uh)],
+            y_send.at[u], y_recv.at[u], hi_peer,
+        )
 
     def d_copy(g, k):
         part = pl.ds(k * gh, gh)
@@ -154,21 +163,27 @@
             d_send.at[2 * g + k], d_recv.at[2 * g + k], lo_peer,
         )
 
-    def fwd(g):
-        for s in range(max(1, g * gs), (g + 1) * gs):
+    def fwd(u):
+        for s in range(max(1, u * hb), (u + 1) * hb):
             a_copy(s).wait_recv()
-        y_copy(g).start()
-        d_copy(g, 0).start()
+        y_copy(u).start()
+        if u % 2:
+            d_copy(u // 2, 0).start()
 
     def rel(g):
-        y_copy(g).wait_recv()
+        y_copy(2 * g).wait_recv()
+        y_copy(2 * g + 1).wait_recv()
         d_copy(g, 1).start()
 
     def e_copy(g):
         return remote(p_oth.at[g], pr.at[g], e_send.at[g], e_recv.at[g], lo_peer)
 
-    def c_copy(g):
-        return remote(p_own.at[g, pl.ds(gh, gh)], yr.at[g], c_send.at[g], c_recv.at[g], hi_peer)
+    def c_copy(u):
+        g, base = u // 2, (u % 2) * uh
+        return remote(
+            p_own.at[g, pl.ds(gh + base, uh)], yr.at[g, pl.ds(base, uh)],
+            c_send.at[u], c_recv.at[u], hi_peer,
+        )
 
     def b_copy(s):
         g, j = s // gs, s % gs
@@ -209,54 +224,72 @@
         e_copy(g).start()
         lower(g, p_own, lo * half)
 
-    def add_into(dst, g, part, src):
+    def add_into(g, part, *others):
         def one(j, carry):
             cols = pl.ds(pl.multiple_of(j * chunk, LANES), chunk)
-            total = dst[g, part, cols].astype(jnp.float32) + src[g, part, cols].astype(jnp.float32)
-            dst[g, part, cols] = total.astype(jnp.bfloat16)
+            total = p_own[g, part, cols].astype(jnp.float32)
+            for other in others:
+                total = total + other[g, part, cols].astype(jnp.float32)
+            p_own[g, part, cols] = total.astype(jnp.bfloat16)
             return carry
 
         lax.fori_loop(0, half // chunk, one, 0)
 
-    def comb1(g):
-        e_copy(g).wait_recv()
-        add_into(p_own, g, slice(gh, 2 * gh), pr)
-        c_copy(g).start()
-        add_into(p_own, g, slice(0, gh), pr)
-
-    def comb2(g):
-        c_copy(g).wait_recv()
-        add_into(p_own, g, slice(0, gh), yr)
-        for s in range(max(1, g * gs), (g + 1) * gs):
+    def comb1(u):
+        base = gh + (u % 2) * uh
+        add_into(u // 2, slice(base, base + uh), pr)
+        c_copy(u).start()
+
+    def comb2(u):
+        base = (u % 2) * uh
+        c_copy(u).wait_recv()
+        add_into(u // 2, slice(base, base + uh), pr, yr)
+        for s in range(max(1, u * hb), (u + 1) * hb):
             b_copy(s).start()
-        if g == 0:
+        if u == 0:
             back[:blk, :] = p_own[0, :blk, :]
 
     fwd(0)
     fwd(1)
+    fwd(2)
+    fwd(3)
     rel(0)
-    rel(1)
     up_copy.wait()
     down_copy.wait()
-    fwd(2)
+    compute(0)
+    fwd(4)
+    project(0)
+    fwd(5)
+    rel(1)
     compute(1)
     project(1)
-    comb1(1)
-    fwd(3)
+    fwd(6)
+    e_copy(1).wait_recv()
+    comb1(2)
     rel(2)
     compute(2)
     project(2)
-    comb2(1)
-    comb1(2)
+    e_copy(2).wait_recv()
+    comb1(4)
+    fwd(7)
+    comb1(5)
+    comb2(2)
+    comb2(4)
     rel(3)
     compute(3)
+    comb2(5)
     project(3)
-    comb2(2)
+    e_copy(3).wait_recv()
+    comb1(6)
+    comb1(7)
     comb1(3)
-    compute(0)
-    project(0)
+    e_copy(0).wait_recv()
+    comb1(1)
     comb1(0)
+    comb2(6)
+    comb2(7)
     comb2(3)
+    comb2(1)
     comb2(0)
 
     for s in range(1, n):
@@ -277,11 +310,13 @@
         a_copy(s).wait_send()
         b_copy(s).wait_send()
     for g in range(GROUPS):
-        y_copy(g).wait_send()
+        y_copy(2 * g).wait_send()
+        y_copy(2 * g + 1).wait_send()
+        c_copy(2 * g).wait_send()
+        c_copy(2 * g + 1).wait_send()
         d_copy(g, 0).wait_send()
         d_copy(g, 1).wait_send()
         e_copy(g).wait_send()
-        c_copy(g).wait_send()
     f_copy.wait()
 
 
@@ -327,10 +362,10 @@
             dma((2,)),
             dma((2,)), dma((2,)),
             dma((n,)), dma((n,)),
+            dma((2 * GROUPS,)), dma((2 * GROUPS,)),
+            dma((2 * GROUPS,)), dma((2 * GROUPS,)),
             dma((GROUPS,)), dma((GROUPS,)),
             dma((2 * GROUPS,)), dma((2 * GROUPS,)),
-            dma((GROUPS,)), dma((GROUPS,)),
-            dma((GROUPS,)), dma((GROUPS,)),
             dma((n,)), dma((n,)),
             dma((1,)), dma((1,)),
         ],
@@ -338,7 +373,7 @@
             collective_id=0, has_side_effects=True, vmem_limit_bytes=67043328
         ),
     )(
-        tokens, node_ids, expert_ids, gate_weights, up_weight,
+        tokens, node_ids.T, expert_ids.T, gate_weights.T, up_weight,
         down_weight.reshape(per_node * unit, model_width),
     )
 

time: 138 us -> 125 us (0.906)
  Pallas kernels: 132 us -> 123 us
  local copies, waits for them, and re-layouts: 6.1 us -> 1.97 us
    pallas_call x1, Pallas kernels: 132 us -> 123 us  [body(): pl.pallas_call(functools.partial(kernel, cfg), out_shape=jax.ShapeDtypeSt...]
    unnamed x4 -> x1, local copies, waits for them, and re-layouts: 6.1 us -> 1.97 us
where the time goes in v2:
time: 125 us
  Pallas kernels  123 us (98%)
  local copies, waits for them, and re-layouts  1.97 us (2%)
    pallas_call x1, Pallas kernels, body(): pl.pallas_call(functools.partial(kernel, cfg), out_shape=jax.ShapeDtypeSt...  123 us

profile of v2, /device:TPU:9, one launch (start us, length us, event | category | flops | bytes accessed | tf_op | source)
XLA Modules:
  0.0 124.6 jit_solution(1571015277071010904)
XLA Ops:
  0.0 122.7 %shard_map.64 = bf16[64,5120]{1,0:T(8,128)(2,1)} custom-call(bf16[64,5120]{1,0:T(8,128)(2,1)} %tok_ref.1, s32[3,64]{1,0:T(4,128)} %bitcast.6, s32[6,64]{1,0:T(8,128)} %bitcast.5, bf16[6,64]{1,0:T(8,128)(2,1)} %bitcast.7, bf16[3,5120,384]{2,1,0:T(8,128)(2,1)} %up_hbm.1, bf16[1152,5120]{1,0:T(8,128)(2,1)} %bitcast.4), custom_call_target="tpu_custom_call" | custom-call | tf_op jit(solution)/shard_map/pallas_call | solution.py:340
  122.7 2.0 %copy.8 = bf16[64,5120]{1,0:T(8,128)(2,1)} copy(bf16[64,5120]{1,0:T(8,128)(2,1)} %shard_map.64) | data formatting | bytes 1310720
